TPU v7x, 16 devices: a 4x2x1 block of a 4x4x4 slice. The times are simulated.
16 devices in a mesh: dp: 4 (over y, z, core), tp: 4 (over x).
Axes of the slice: x: 4, y: 2, z: 1, core: 2. Of those that a mesh axis runs over, the one named last changes fastest.
The devices are a block of a 4x4x4 slice.
Arguments:
- x: bfloat16 [8192, 8192], P('dp'), parts along dimension 0
- w_gate: bfloat16 [8192, 32768], P(None, 'tp')
- w_up: bfloat16 [8192, 32768], P(None, 'tp')
- w_down: bfloat16 [32768, 8192], P('tp')
Outputs:
- output: bfloat16 [8192, 8192], P('dp'), parts along dimension 0
There are 4 independent parts. A program takes and returns all parts, laid end to end along the dimension named above; an argument that names none is the same for every part.
All inputs are finite; a program needn't handle non-finite values.
Results may differ from a plain program's by a relative error of at most 0.016.
Values are sent between devices in bfloat16 or wider.
A program may use at most 1.5 GiB of HBM per device.

v0:
```python
import jax
import jax.numpy as jnp
from jax import lax
from jax.sharding import PartitionSpec as P


def solution(mesh):
    def step(x, w_gate, w_up, w_down):
        gate = jnp.dot(x, w_gate, preferred_element_type=jnp.float32)
        up = jnp.dot(x, w_up, preferred_element_type=jnp.float32)
        hidden = (jax.nn.silu(gate) * up).astype(jnp.bfloat16)
        term = jnp.dot(hidden, w_down, preferred_element_type=jnp.float32).astype(jnp.bfloat16)
        return lax.psum(term, "tp")

    return jax.shard_map(
        step,
        mesh=mesh,
        in_specs=(P("dp", None), P(None, "tp"), P(None, "tp"), P("tp", None)),
        out_specs=P("dp", None),
        check_vma=False,
    )
```

profile of v0, /device:TPU:112, one launch (start us, length us, event | category | flops | bytes accessed | tf_op | source)
XLA Modules:
  0.0 1524.1 jit_solution(14695543527040610485)
XLA Ops:
  6.5 0.0 all-reduce.2.cloned.1.call-start
  6.6 304.5 %fusion = f32[2048,8192]{1,0:T(8,128)} fusion(bf16[2048,8192]{1,0:T(8,128)(2,1)} %param.4, bf16[8192,8192]{1,0:T(8,128)(2,1)} %param.5), kind=kOutput, calls=%fused_computation.2 | convolution fusion | flops 274877906944 | bytes 234881024 | tf_op jit(solution)/shard_map/dot_general | solution.py:9
  311.0 314.4 %multiply_convert_fusion = bf16[2048,8192]{1,0:T(8,128)(2,1)} fusion(f32[2048,8192]{1,0:T(8,128)} %fusion, bf16[2048,8192]{1,0:T(8,128)(2,1)} %param.4, bf16[8192,8192]{1,0:T(8,128)(2,1)} %param.6), kind=kOutput, calls=%fused_computation | convolution fusion | flops 274978570240 | bytes 268435456 | tf_op jit(solution)/shard_map/dot_general | solution.py:10
  625.4 309.0 %convolution_convert_fusion = bf16[2048,8192]{1,0:T(8,128)(2,1)} fusion(bf16[2048,8192]{1,0:T(8,128)(2,1)} %multiply_convert_fusion, bf16[8192,8192]{1,0:T(8,128)(2,1)} %param.7), kind=kOutput, calls=%fused_computation.1 | convolution fusion | flops 274894684160 | bytes 201326592 | tf_op jit(solution)/shard_map/dot_general | solution.py:12
  934.3 0.1 all-reduce.2.cloned.1.call-update
  934.4 559.9 %all-reduce.2.cloned.1.call-done = bf16[2048,8192]{1,0:T(8,128)(2,1)} async-done(((bf16[2048,8192]{1,0:T(8,128)(2,1)}), bf16[2048,8192]{1,0:T(8,128)(2,1)}) %all-reduce.2.cloned.1.call-update) | async-done | bytes 33554448 | tf_op jit(solution)/shard_map/psum | solution.py:13
  1494.3 23.0 %copy.6 = bf16[2048,8192]{1,0:T(8,128)(2,1)} copy(bf16[2048,8192]{1,0:T(8,128)(2,1)} %all-reduce.2.cloned.1.call-done) | data formatting | bytes 67108864
Async XLA Ops:
  6.5 1487.7 %all-reduce.2.cloned.1.call-start = ((), (), s32[]{:S(2)}) async-start(), calls=%async_computation | async-start | bytes 67108864 | tf_op jit(solution)/shard_map/psum | solution.py:13
Sparse Core Ops, SparseCore 0:
  934.5 559.7 all-reduce.1
where the time goes:
time: 1520 us
  matrix products  928 us (61%)
  waiting for transfers between devices  560 us (37%)
  local copies, waits for them, and re-layouts  23 us (2%)
    psum x1, waiting for transfers between devices, step(): return lax.psum(term, 'tp')  560 us
    dot_general x1, matrix products, step(): up = jnp.dot(x, w_up, preferred_element_type=jnp.float32)  314 us
    dot_general x1, matrix products, step(): jnp.dot(hidden, w_down, preferred_element_type=jnp.float32)  309 us
    dot_general x1, matrix products, step(): gate = jnp.dot(x, w_gate, preferred_element_type=jnp.float32)  304 us
  transfers between devices with their start and end apart: 1, of which 1 were waited for; matrix products, arithmetic and copies ran while one was open for 0% of the time, Pallas kernels for 0%

commit v1 on v0

v1 whole, which is shorter than its diff:
```python
import functools

import jax
import jax.numpy as jnp
from jax import lax
from jax.experimental import pallas as pl
from jax.experimental.pallas import tpu as pltpu
from jax.sharding import PartitionSpec as P

MESH = pl.DeviceIdType.MESH
BF16, F32 = jnp.bfloat16, jnp.float32
COL = 256
SLOTS = 4
STAGE = 4
RING = 6
SENDS = 4
LARGE, COUNT = 448, 4


def products(lhs, wv, slot):
    K = wv.shape[2]
    out = [None, None]
    for k in range(K // COL):
        at = pl.ds(k * COL, COL)
        a = lhs(at)
        for i in range(2):
            v = jnp.dot(a, wv[slot, i, at, :], preferred_element_type=F32)
            out[i] = v if k == 0 else out[i] + v
    return out


def kernel(nt, large, count, x, wg, wu, wd, y, xv, hv, wv, rsin, stg, wsem, xsem, rssend, rsrecv, credit, agrecv, agsend, lsem):
    rows, K = x.shape
    small = rows - large * count
    part = y.shape[1] // (2 * nt)
    nb = part // COL
    dn, gn = nt * nb, wg.shape[1] // COL
    drounds, rounds = dn // 2, gn // 2
    phase = dn + gn
    total = gn + count * phase + dn
    rsn = dn - nb

    me = lax.axis_index("tp")
    right, left = lax.rem(me + 1, nt), lax.rem(me + nt - 1, nt)
    ahead, behind = (right, left), (left, right)

    barrier = pltpu.get_barrier_semaphore()
    for other in (left, right):
        pl.semaphore_signal(barrier, inc=1, device_id={"tp": other}, device_id_type=MESH)
    pl.semaphore_wait(barrier, 2)

    def col_of(way, hop, b):
        owner = lax.rem(me - hop + nt, nt) if way == 0 else lax.rem(me + hop, nt)
        return pl.multiple_of(way * (part * nt) + owner * part + b * COL, COL)

    def w_start(t):
        slot = lax.rem(t, SLOTS)
        rho = lax.rem(jnp.maximum(t - gn, 0), phase)
        q, r = rho // 4, lax.rem(rho, 4)
        last = t >= gn + count * phase
        down = last | ((t >= gn) & (rho < 4 * drounds) & (r < 2))
        ds = jnp.where(last, t - gn - count * phase, 2 * q + r)
        j = jnp.where(t < gn, t, jnp.where(rho < 4 * drounds, 2 * q + r - 2, rho - dn))

        @pl.when(down & (t < total))
        def _():
            a, b = ds // nb, lax.rem(ds, nb)
            for way in range(2):
                src = wd.at[:, pl.ds(col_of(way, a + 1, b), COL)]
                pltpu.make_async_copy(src, wv.at[slot, way], wsem.at[slot, way]).start()

        @pl.when(jnp.logical_not(down))
        def _():
            c = pl.ds(pl.multiple_of(j * COL, COL), COL)
            for i, w in enumerate((wg, wu)):
                pltpu.make_async_copy(w.at[:, c], wv.at[slot, i], wsem.at[slot, i]).start()

    def w_wait(t):
        slot = lax.rem(t, SLOTS)
        for i in range(2):
            pltpu.make_async_copy(wg.at[:, pl.ds(0, COL)], wv.at[slot, i], wsem.at[slot, i]).wait()

    def x_copy(row, m):
        return pltpu.make_async_copy(x.at[pl.ds(row, m), :], xv.at[pl.ds(0, m), :], xsem)

    def rs_copy(way, m, s, slot):
        return pltpu.make_async_remote_copy(
            src_ref=stg.at[way, s, pl.ds(0, m)], dst_ref=rsin.at[way, slot, pl.ds(0, m)],
            send_sem=rssend.at[way, s], recv_sem=rsrecv.at[way, slot],
            device_id={"tp": ahead[way]}, device_id_type=MESH)

    def y_at(way, hop, row, m, b):
        return y.at[pl.ds(row, m), pl.ds(col_of(way, hop, b), COL)]

    def y_own(way, m, s, row, b):
        return pltpu.make_async_copy(stg.at[way, s, pl.ds(0, m)], y_at(way, 0, row, m, b), lsem.at[way, s])

    def ag_first(way, m, s, row, b, c):
        return pltpu.make_async_remote_copy(
            src_ref=stg.at[way, s, pl.ds(0, m)], dst_ref=y_at(way, 0, row, m, b),
            send_sem=rssend.at[way, s], recv_sem=agrecv.at[way, 0, c * nb + b],
            device_id={"tp": ahead[way]}, device_id_type=MESH)

    def ag_copy(way, hop, m, row, b, c, f, recv):
        at = y_at(way, hop, row, m, b)
        return pltpu.make_async_remote_copy(
            src_ref=at, dst_ref=at, send_sem=agsend.at[way, f], recv_sem=agrecv.at[way, recv, c * nb + b],
            device_id={"tp": ahead[way]}, device_id_type=MESH)

    def forward(c, row, m, ev, m_before):
        hop, b = 1 + ev // nb, lax.rem(ev, nb)
        n = c * (nt - 2) * nb + ev
        f = lax.rem(n, SENDS)

        @pl.when(n >= SENDS)
        def _():
            for way in range(2):
                ag_copy(way, 1, m_before, 0, 0, 0, f, 0).wait_send()

        for way in range(2):
            ag_copy(way, hop, m, row, b, c, f, hop - 1).wait_recv()
            ag_copy(way, hop, m, row, b, c, f, hop).start()

    def gate_up(m, t, n, hs, j):
        for k in range(n):
            w_wait(t + k)
        for k in range(n):
            slot = lax.rem(t + k, SLOTS)
            g, u = products(lambda at: xv[pl.ds(0, m), at], wv, slot)
            at = pl.ds(pl.multiple_of((j + k) * COL, COL), COL)
            hv[hs, pl.ds(0, m), at] = (jax.nn.silu(g) * u).astype(BF16)
        for k in range(n):
            w_start(t + SLOTS + k)

    def down(m, t, n, hs, c, ds, m_before):
        for k in range(n):
            w_wait(t + k)
        dc = c * dn + ds

        @pl.when(dc >= STAGE)
        def _():
            for k in range(n):
                s = lax.rem(dc + k, STAGE)
                for way in range(2):
                    rs_copy(way, m_before, s, 0).wait_send()

        @pl.when((c >= 1) & (ds < nb))
        def _():
            for k in range(n):
                s = lax.rem(dc + k, STAGE)
                for way in range(2):
                    y_own(way, m_before, s, 0, 0).wait()

        @pl.when(ds >= nb)
        def _():
            for k in range(n):
                for way in range(2):
                    rs_copy(way, m, 0, lax.rem(c * rsn + ds - nb + k, RING)).wait_recv()

        for k in range(n):
            slot, s = lax.rem(t + k, SLOTS), lax.rem(dc + k, STAGE)
            came = jnp.where(ds >= nb, lax.rem(jnp.maximum(c * rsn + ds - nb + k, 0), RING), RING)
            both = products(lambda at: hv[hs, pl.ds(0, m), at], wv, slot)
            for way in range(2):
                v = both[way]
                v = v + rsin[way, came, pl.ds(0, m), :].astype(F32)
                stg[way, s, pl.ds(0, m), :] = v.astype(BF16)
        for k in range(n):
            w_start(t + SLOTS + k)

    def send(m, n, c, row, ds):
        dc, so = c * dn + ds, c * rsn + ds

        @pl.when((ds >= nb) & (so - nb + RING < (count + 1) * rsn))
        def _():
            for way in range(2):
                for k in range(n):
                    @pl.when(so - nb + k + RING < (count + 1) * rsn)
                    def _():
                        pl.semaphore_signal(credit.at[way], inc=1, device_id={"tp": behind[way]}, device_id_type=MESH)

        @pl.when(ds < rsn)
        def _():
            for k in range(n):
                @pl.when(so + k >= RING)
                def _():
                    for way in range(2):
                        pl.semaphore_wait(credit.at[way], 1)

                for way in range(2):
                    rs_copy(way, m, lax.rem(dc + k, STAGE), lax.rem(so + k, RING)).start()

        @pl.when(ds >= rsn)
        def _():
            for k in range(n):
                s, b = lax.rem(dc + k, STAGE), ds - rsn + k
                for way in range(2):
                    ag_first(way, m, s, row, b, c).start()
                    y_own(way, m, s, row, b).start()

    def row_of(c):
        return pl.multiple_of(c * large, 16)

    x_copy(0, large).start()
    for s in range(SLOTS):
        w_start(jnp.int32(s))
    rsin[:, RING] = jnp.zeros_like(rsin[:, RING])
    x_copy(0, large).wait()

    def large_round(n, _):
        i, q = n // rounds, lax.rem(n, rounds)
        t = jnp.where(i == 0, 2 * q, gn + (i - 1) * phase + jnp.where(q < drounds, 4 * q, dn + 2 * q))
        has_down = (i > 0) & (q < drounds)

        @pl.when((i > 0) & (q == 0))
        def _():
            x_copy(row_of(i), large).start()

        @pl.when(has_down)
        def _():
            down(large, t, 2, lax.rem(i + 1, 2), i - 1, 2 * q, large)
            send(large, 2, i - 1, row_of(i - 1), 2 * q)

        @pl.when((i > 0) & (q == 0))
        def _():
            x_copy(row_of(i), large).wait()

        @pl.when((i > 0) & (q >= drounds) & (q - drounds < (nt - 2) * nb))
        def _():
            forward(i - 1, row_of(i - 1), large, q - drounds, large)

        gate_up(large, jnp.where(has_down, t + 2, t), 2, lax.rem(i, 2), 2 * q)
        return 0

    lax.fori_loop(0, count * rounds, large_round, 0)

    t0, c0 = gn + (count - 1) * phase, count - 1
    hs0, hs1 = c0 % 2, count % 2
    x_copy(count * large, small).start()

    def small_round(q, _):
        t = t0 + jnp.where(q < drounds, 4 * q, dn + 2 * q)

        @pl.when(q < drounds)
        def _():
            down(large, t, 2, hs0, c0, 2 * q, large)
            send(large, 2, c0, c0 * large, 2 * q)

        @pl.when(q == 0)
        def _():
            x_copy(count * large, small).wait()

        @pl.when((q >= drounds) & (q - drounds < (nt - 2) * nb))
        def _():
            forward(c0, c0 * large, large, q - drounds, large)

        def one(k, _):
            gate_up(small, jnp.where(q < drounds, t + 2, t) + k, 1, hs1, 2 * q + k)
            return 0

        lax.fori_loop(0, 2, one, 0)
        return 0

    lax.fori_loop(0, rounds, small_round, 0)

    def last_round(ds, _):
        t = t0 + phase + ds
        first = nb

        @pl.when(ds < first)
        def _():
            before(ds, large)

        @pl.when(ds >= first)
        def _():
            before(ds, small)

        down_last(t, ds)
        send(small, 1, count, count * large, ds)
        return 0

    def before(ds, m):
        s = lax.rem(count * dn + ds, STAGE)
        for way in range(2):
            rs_copy(way, m, s, 0).wait_send()

    def down_last(t, ds):
        w_wait(t)
        c = count
        dc = c * dn + ds
        slot, s = lax.rem(t, SLOTS), lax.rem(dc, STAGE)

        @pl.when(ds < nb)
        def _():
            for way in range(2):
                y_own(way, large, s, 0, 0).wait()

        @pl.when(ds >= nb)
        def _():
            for way in range(2):
                rs_copy(way, small, 0, lax.rem(c * rsn + ds - nb, RING)).wait_recv()

        came = jnp.where(ds >= nb, lax.rem(c * rsn + ds - nb, RING), RING)
        both = products(lambda at: hv[hs1, pl.ds(0, small), at], wv, slot)
        for way in range(2):
            v = both[way]
            v = v + rsin[way, came, pl.ds(0, small), :].astype(F32)
            stg[way, s, pl.ds(0, small), :] = v.astype(BF16)
        w_start(t + SLOTS)

    lax.fori_loop(0, dn, last_round, 0)

    for ev in range((nt - 2) * nb):
        forward(count, count * large, small, jnp.int32(ev), large if ev < SENDS else small)
    for b in range(nb):
        s = (count * dn + rsn + b) % STAGE
        for way in range(2):
            rs_copy(way, small, s, 0).wait_send()
            y_own(way, small, s, 0, 0).wait()
    for f in range(SENDS):
        for way in range(2):
            ag_copy(way, 1, small, 0, 0, 0, f, 0).wait_send()
    for c in range(count + 1):
        m = large if c < count else small
        for b in range(nb):
            for way in range(2):
                ag_copy(way, nt - 1, m, c * large, b, c, 0, nt - 2).wait_recv()


def block(nt, large, count, x, wg, wu, wd):
    rows, K = x.shape
    nb = wd.shape[1] // (2 * nt * COL)
    assert STAGE == nb and (nt - 2) * nb >= SENDS and wg.shape[1] == K and wd.shape[0] == K
    return pl.pallas_call(
        functools.partial(kernel, nt, large, count),
        out_shape=jax.ShapeDtypeStruct((rows, wd.shape[1]), BF16),
        in_specs=[pl.BlockSpec(memory_space=pl.ANY)] * 4,
        out_specs=pl.BlockSpec(memory_space=pl.ANY),
        scratch_shapes=[
            pltpu.VMEM((large, K), BF16),
            pltpu.VMEM((2, large, K), BF16),
            pltpu.VMEM((SLOTS, 2, K, COL), BF16),
            pltpu.VMEM((2, RING + 1, large, COL), BF16),
            pltpu.VMEM((2, STAGE, large, COL), BF16),
            pltpu.SemaphoreType.DMA((SLOTS, 2)),
            pltpu.SemaphoreType.DMA,
            pltpu.SemaphoreType.DMA((2, STAGE)),
            pltpu.SemaphoreType.DMA((2, RING)),
            pltpu.SemaphoreType.REGULAR((2,)),
            pltpu.SemaphoreType.DMA((2, nt - 1, (count + 1) * nb)),
            pltpu.SemaphoreType.DMA((2, SENDS)),
            pltpu.SemaphoreType.DMA((2, STAGE)),
        ],
        compiler_params=pltpu.CompilerParams(collective_id=0, has_side_effects=True, vmem_limit_bytes=67043328),
        name="mlp_block",
    )(x, wg, wu, wd)


def solution(mesh):
    nt = mesh.shape["tp"]
    return jax.shard_map(
        functools.partial(block, nt, LARGE, COUNT),
        mesh=mesh,
        in_specs=(P("dp", None), P(None, "tp"), P(None, "tp"), P("tp", None)),
        out_specs=P("dp", None),
        check_vma=False,
    )
```

time: 1520 us -> 949 us (0.62)
  matrix products: 928 us -> 0 us
  Pallas kernels: 0 us -> 926 us
  waiting for transfers between devices: 560 us -> 0 us
    dot_general x3 -> x0, matrix products: 928 us -> none  [the longest x1 314 us: step(): up = jnp.dot(x, w_up, preferred_element_type=jnp.float32)]
    pallas_call x0 -> x1, Pallas kernels: none -> 926 us  [block(): pl.pallas_call(functools.partial(kernel, nt, large, count), out_shape=jax...]
    psum x1 -> x0, waiting for transfers between devices: 560 us -> none  [step(): return lax.psum(term, 'tp')]
  transfers between devices with their start and end apart: 1 -> 0, of which waited for: 1 -> 0; matrix products, arithmetic and copies ran while one was open for 0% -> 0% of each run, Pallas kernels for 0% -> 0%
where the time goes in v1:
time: 949 us
  Pallas kernels  926 us (98%)
  local copies, waits for them, and re-layouts  23 us (2%)
    pallas_call x1, Pallas kernels, block(): pl.pallas_call(functools.partial(kernel, nt, large, count), out_shape=jax...  926 us
    unnamed x1, local copies, waits for them, and re-layouts  23 us

profile of v1, /device:TPU:112, one launch (start us, length us, event | category | flops | bytes accessed | tf_op | source)
XLA Modules:
  0.0 948.9 jit_solution(720360440301793690)
XLA Ops:
  0.0 925.9 %mlp_block.1 = bf16[2048,8192]{1,0:T(8,128)(2,1)} custom-call(bf16[2048,8192]{1,0:T(8,128)(2,1)} %x.1, bf16[8192,8192]{1,0:T(8,128)(2,1)} %wg.1, bf16[8192,8192]{1,0:T(8,128)(2,1)} %wu.1, bf16[8192,8192]{1,0:T(8,128)(2,1)} %wd.1), custom_call_target="tpu_custom_call" | custom-call | tf_op jit(solution)/shard_map/mlp_block/pallas_call | solution.py:334
  925.9 23.0 %copy.6 = bf16[2048,8192]{1,0:T(8,128)(2,1)} copy(bf16[2048,8192]{1,0:T(8,128)(2,1)} %mlp_block.1) | data formatting | bytes 67108864

commit v2 on v0

v2 whole, which is shorter than its diff:
```python
import functools

import jax
import jax.numpy as jnp
from jax import lax
from jax.experimental import pallas as pl
from jax.experimental.pallas import tpu as pltpu
from jax.sharding import PartitionSpec as P

MESH = pl.DeviceIdType.MESH
BF16, F32 = jnp.bfloat16, jnp.float32
COL = 256
WIDE = 2 * COL
SLOTS = 4
LARGE, COUNT = 448, 4


def kernel(nt, large, count, x, wg, wu, wd, y, wv, xv, hv, rsin, stg, wsem, xsem,
           rssend, rsrecv, agrecv, agsend, lsem, srssend, srsrecv, sagrecv, sagsend, slsem, vsem):
    rows, K = x.shape
    small = rows - large * count
    part = y.shape[1] // (2 * nt)
    nb = part // COL
    lag = nb // 2
    ring = 2 * lag
    dn, gn = nt * nb, wg.shape[1] // COL
    drounds = dn // 2
    phase = dn + gn
    total = gn + count * phase + dn
    rsn = drounds - lag
    hops = nt - 1

    me = lax.axis_index("tp")
    right, left = lax.rem(me + 1, nt), lax.rem(me + nt - 1, nt)
    ahead = (right, left)

    def col_of(way, hop, c):
        owner = lax.rem(me - hop + 2 * nt, nt) if way == 0 else lax.rem(me + hop, nt)
        return pl.multiple_of(way * (part * nt) + owner * part + c, COL)

    def w_start(t):
        slot = lax.rem(t, SLOTS)
        u = jnp.maximum(t - gn, 0)
        i = jnp.minimum(u // phase, count)
        rho = u - i * phase
        turn = jnp.where(i == count - 1, 3, 4)
        q, last = rho // turn, i == count
        r = rho - q * turn
        mixed = q < drounds
        down = last | ((t >= gn) & mixed & (r < 2))
        ds = jnp.minimum(jnp.where(last, rho, 2 * q + r), dn - 1)
        j = jnp.where(t < gn, t, jnp.where(mixed, (turn - 2) * q + r - 2, rho - dn))

        @pl.when(down & (t <= total))
        def _():
            a, b = ds // nb, lax.rem(ds, nb)
            for way in range(2):
                src = wd.at[:, pl.ds(col_of(way, a + 1, b * COL), COL)]
                pltpu.make_async_copy(src, wv.at[slot, way], wsem.at[slot, way]).start()

        @pl.when(jnp.logical_not(down))
        def _():
            c = pl.ds(pl.multiple_of(j * COL, COL), COL)
            for i, w in enumerate((wg, wu)):
                pltpu.make_async_copy(w.at[:, c], wv.at[slot, i], wsem.at[slot, i]).start()

    def w_wait(t):
        slot = lax.rem(t, SLOTS)
        for i in range(2):
            pltpu.make_async_copy(wg.at[:, pl.ds(0, COL)], wv.at[slot, i], wsem.at[slot, i]).wait()

    def x_copy(row, m):
        return pltpu.make_async_copy(x.at[pl.ds(row, m), :], xv.at[pl.ds(0, m), :], xsem)

    def remote(way, src, dst, send_sem, recv_sem):
        return pltpu.make_async_remote_copy(
            src_ref=src, dst_ref=dst, send_sem=send_sem, recv_sem=recv_sem,
            device_id={"tp": ahead[way]}, device_id_type=MESH)

    def rs_copy(way, s, slot):
        return remote(way, stg.at[way, s], rsin.at[way, slot], rssend.at[way, s], rsrecv.at[way, slot])

    def y_at(way, hop, c, f):
        return y.at[pl.ds(pl.multiple_of(c * large, 16), large), pl.ds(col_of(way, hop, f * WIDE), WIDE)]

    def y_own(way, s, c, f):
        return pltpu.make_async_copy(stg.at[way, s], y_at(way, 0, c, f), lsem.at[way, s])

    def ag_first(way, s, c, f):
        return remote(way, stg.at[way, s], y_at(way, 0, c, f), rssend.at[way, s], agrecv.at[way, 0, c * lag + f])

    def ag_copy(way, hop, c, f, s, recv):
        at = y_at(way, hop, c, f)
        return remote(way, at, at, agsend.at[way, s], agrecv.at[way, recv, c * lag + f])

    def forward(c, ev, on):
        hop, f = 1 + ev // lag, lax.rem(ev, lag)
        n = c * (nt - 2) * lag + ev
        s = lax.rem(n, 2)
        for way in range(2):
            @pl.when(on & (n >= 2))
            def _():
                ag_copy(way, 1, 0, 0, s, 0).wait_send()

            @pl.when(on)
            def _():
                ag_copy(way, hop, c, f, s, hop - 1).wait_recv()

            @pl.when(on)
            def _():
                ag_copy(way, hop, c, f, s, hop).start()

    def half(h):
        return pl.ds(pl.multiple_of(h * COL, COL), COL)

    def small_rs(way, s, h, slot):
        return remote(way, stg.at[way, s, pl.ds(0, small), half(h)], rsin.at[way, slot, pl.ds(0, small), half(h)],
                      srssend.at[way, 2 * s + h], srsrecv.at[way, 2 * slot + h])

    def small_y(way, hop, b):
        return y.at[pl.ds(large * count, small), pl.ds(col_of(way, hop, b * COL), COL)]

    def small_own(way, s, h, b):
        return pltpu.make_async_copy(stg.at[way, s, pl.ds(0, small), half(h)], small_y(way, 0, b), slsem.at[way, 2 * s + h])

    def small_first(way, s, h, b):
        return remote(way, stg.at[way, s, pl.ds(0, small), half(h)], small_y(way, 0, b),
                      srssend.at[way, 2 * s + h], sagrecv.at[way, 0, b])

    def small_ag(way, hop, b, s, recv):
        at = small_y(way, hop, b)
        return remote(way, at, at, sagsend.at[way, s], sagrecv.at[way, recv, b])

    def products(lhs, t, beside):
        slot = lax.rem(t, SLOTS)
        beside = [(K // COL // 4, lambda: w_start(t + 3)), (3 * (K // COL) // 4, lambda: w_wait(t + 1)), *beside]
        out = [None, None]
        for k in range(K // COL):
            at = pl.ds(k * COL, COL)
            a = lhs(at)
            for i in range(2):
                v = jnp.dot(a, wv[slot, i, at, :], preferred_element_type=F32)
                out[i] = v if k == 0 else out[i] + v
            for when, act in beside:
                if when == k:
                    act()
        return out

    mid = K // COL // 2

    def gate_up(m, t, hs, j, *beside):
        g, u = products(lambda at: xv[pl.ds(0, m), at], t, beside)
        hv[hs, pl.ds(0, m), pl.ds(pl.multiple_of(j * COL, COL), COL)] = (jax.nn.silu(g) * u).astype(BF16)

    def down_pair(t, hs, c, q, beside):
        s = lax.rem(c * drounds + q, lag)
        came = lax.rem(jnp.maximum(c * rsn + q - lag, 0), ring)
        place = jnp.where(q >= lag, came, ring)

        def ready():
            for way in range(2):
                @pl.when(c * drounds + q >= lag)
                def _():
                    rs_copy(way, s, 0).wait_send()

                @pl.when((c >= 1) & (q < lag))
                def _():
                    y_own(way, s, 0, 0).wait()

                @pl.when(q >= lag)
                def _():
                    rs_copy(way, 0, came).wait_recv()

        for k in range(2):
            both = products(lambda at: hv[hs, :, at], t + k, [(mid, ready)] if k == 0 else beside)
            at = pl.ds(k * COL, COL)
            for way in range(2):
                v = both[way] + rsin[way, place, :, at].astype(F32)
                stg[way, s, :, at] = v.astype(BF16)

    def send(c, q):
        s = lax.rem(c * drounds + q, lag)
        slot = lax.rem(c * rsn + q, ring)
        for way in range(2):
            @pl.when(q < rsn)
            def _():
                rs_copy(way, s, slot).start()

            @pl.when(q >= rsn)
            def _():
                ag_first(way, s, c, q - rsn).start()

            @pl.when(q >= rsn)
            def _():
                y_own(way, s, c, q - rsn).start()

    w_start(jnp.int32(0))
    x_copy(0, large).start()
    barrier = pltpu.get_barrier_semaphore()
    for other in (left, right):
        pl.semaphore_signal(barrier, inc=1, device_id={"tp": other}, device_id_type=MESH)
    pl.semaphore_wait(barrier, 2)
    w_start(jnp.int32(1))
    rsin[:, ring] = jnp.zeros_like(rsin[:, ring])
    x_copy(0, large).wait()
    w_wait(jnp.int32(0))
    w_start(jnp.int32(2))

    first, each = gn // 4, phase // 4

    def large_steps(v, _):
        i = jnp.where(v < first, 0, 1 + (v - first) // each)
        z = jnp.where(v < first, v + drounds, lax.rem(jnp.maximum(v - first, 0), each))
        t = 4 * v
        hs = lax.rem(i, 2)

        @pl.when(z < drounds)
        def _():
            @pl.when(z == 0)
            def _():
                x_copy(pl.multiple_of(i * large, 16), large).start()

            def x_wait():
                pl.when(z == 0)(lambda: x_copy(0, large).wait())

            down_pair(t, 1 - hs, i - 1, z, [(mid, x_wait)])
            gate_up(large, t + 2, hs, 2 * z, (mid, lambda: send(i - 1, z)))
            gate_up(large, t + 3, hs, 2 * z + 1)

        @pl.when(z >= drounds)
        def _():
            j = jnp.where(v < first, 4 * v, 4 * z - dn)
            ev = z - drounds
            on = (v >= first) & (ev < (nt - 2) * lag)
            gate_up(large, t, hs, j, (mid, lambda: forward(i - 1, ev, on)))
            for k in range(1, 4):
                gate_up(large, t + k, hs, j + k)

        return 0

    lax.fori_loop(0, first + each * (count - 1), large_steps, 0)

    t0, c0 = gn + (count - 1) * phase, count - 1
    hs0, hs1 = c0 % 2, count % 2
    x_copy(count * large, small).start()

    def mixed_steps(q, _):
        t = t0 + 3 * q

        def x_wait():
            pl.when(q == 0)(lambda: x_copy(0, small).wait())

        down_pair(t, hs0, c0, q, [(mid, x_wait)])
        gate_up(small, t + 2, hs1, q, (mid, lambda: send(c0, q)))
        return 0

    lax.fori_loop(0, drounds, mixed_steps, 0)

    def small_steps(n, _):
        j = drounds + 2 * n
        on = (lax.rem(n, 3) == 0) & (n // 3 < (nt - 2) * lag)
        gate_up(small, t0 + dn + j, hs1, j, (mid, lambda: forward(c0, n // 3, on)))
        gate_up(small, t0 + dn + j + 1, hs1, j + 1)
        return 0

    lax.fori_loop(0, (gn - drounds) // 2, small_steps, 0)

    t0 += phase

    def last_steps(ds, _):
        q, h = ds // 2, lax.rem(ds, 2)
        s = lax.rem(count * drounds + q, lag)
        came = lax.rem(count * rsn + jnp.maximum(q - lag, 0), ring)
        place = jnp.where(ds >= nb, came, ring)

        def ready():
            for way in range(2):
                @pl.when((q < lag) & (h == 0))
                def _():
                    rs_copy(way, s, 0).wait_send()
                    y_own(way, s, 0, 0).wait()

                @pl.when(ds >= nb)
                def _():
                    small_rs(way, s, h, 0).wait_send()

                @pl.when(ds >= nb)
                def _():
                    small_rs(way, 0, h, came).wait_recv()

        both = products(lambda at: hv[hs1, pl.ds(0, small), at], t0 + ds, [(3 * mid // 2, ready)])
        for way in range(2):
            v = both[way] + rsin[way, place, pl.ds(0, small), half(h)].astype(F32)
            stg[way, s, pl.ds(0, small), half(h)] = v.astype(BF16)
        slot, b = lax.rem(count * rsn + q, ring), ds - 2 * rsn

        @pl.when(ds < 2 * rsn)
        def _():
            for way in range(2):
                small_rs(way, s, h, slot).start()

        @pl.when(ds >= 2 * rsn)
        def _():
            for way in range(2):
                small_first(way, s, h, b).start()
                small_own(way, s, h, b).start()

        return 0

    lax.fori_loop(0, dn, last_steps, 0)

    for n in range(count * lag):
        for way in range(2):
            ag_copy(way, hops, n // lag, n % lag, 0, hops - 1).wait_recv()

    def keep(b):
        src = y.at[pl.ds(0, large * count), pl.ds(b * COL, COL)]
        return pltpu.make_async_copy(src, column(wv, b, large * count, rows), vsem.at[b])

    for b in range(y.shape[1] // COL):
        keep(b).start()

    for ev in range((nt - 2) * nb):
        hop, b = 1 + ev // nb, ev % nb
        for way in range(2):
            if ev >= nb:
                small_ag(way, 1, 0, b, 0).wait_send()
            small_ag(way, hop, b, b, hop - 1).wait_recv()
            small_ag(way, hop, b, b, hop).start()
    for way in range(2):
        for b in range(nb):
            small_rs(way, b // 2, b % 2, 0).wait_send()
            small_own(way, b // 2, b % 2, 0).wait()
            small_ag(way, 1, 0, b, 0).wait_send()
        for s in range(2):
            ag_copy(way, 1, 0, 0, s, 0).wait_send()
    for b in range(y.shape[1] // COL):
        keep(b).wait()
    for way in range(2):
        for b in range(nb):
            small_ag(way, hops, b, 0, hops - 1).wait_recv()


def column(v, b, rows, whole):
    per = v.shape[2] // whole
    return v.at[b // (2 * per), (b // per) % 2, pl.ds(b % per * whole, rows), :]


def lay_out(done, y, v, out, tail, sem, sems):
    rows, n = out.shape[0], out.shape[1] // COL
    rest = pltpu.make_async_copy(y.at[pl.ds(done, rows - done), :], tail, sem)
    rest.start()

    def copy(b):
        return pltpu.make_async_copy(column(v, b, done, rows), out.at[pl.ds(0, done), pl.ds(b * COL, COL)], sems.at[b])

    for b in range(n):
        copy(b).start()
    rest.wait()
    rest = pltpu.make_async_copy(tail, out.at[pl.ds(done, rows - done), :], sem)
    rest.start()
    for b in range(n):
        copy(b).wait()
    rest.wait()


def block(nt, large, count, x, wg, wu, wd):
    rows, K = x.shape
    nb = wd.shape[1] // (2 * nt * COL)
    lag = nb // 2
    assert wg.shape[1] == K and wd.shape[0] == K and wd.shape[1] == K and count * (nt - 2) * lag >= 2
    dma = pltpu.SemaphoreType.DMA
    y, v = pl.pallas_call(
        functools.partial(kernel, nt, large, count),
        out_shape=[jax.ShapeDtypeStruct((rows, wd.shape[1]), BF16), pltpu.VMEM((SLOTS, 2, K, COL), BF16)],
        in_specs=[pl.BlockSpec(memory_space=pl.ANY)] * 4,
        out_specs=[pl.BlockSpec(memory_space=pl.ANY), pl.BlockSpec(memory_space=pltpu.VMEM)],
        scratch_shapes=[
            pltpu.VMEM((large, K), BF16),
            pltpu.VMEM((2, large, K), BF16),
            pltpu.VMEM((2, 2 * lag + 1, large, WIDE), BF16),
            pltpu.VMEM((2, lag, large, WIDE), BF16),
            dma((SLOTS, 2)), dma,
            dma((2, lag)), dma((2, 2 * lag)), dma((2, nt - 1, count * lag)), dma((2, 2)), dma((2, lag)),
            dma((2, nb)), dma((2, 2 * nb)), dma((2, nt - 1, nb)), dma((2, nb)), dma((2, nb)), dma((wd.shape[1] // COL,)),
        ],
        compiler_params=pltpu.CompilerParams(collective_id=0, has_side_effects=True, vmem_limit_bytes=30 * 2**20),
        name="mlp_block",
    )(x, wg, wu, wd)
    return pl.pallas_call(
        functools.partial(lay_out, large * count),
        out_shape=jax.ShapeDtypeStruct((rows, wd.shape[1]), BF16),
        in_specs=[pl.BlockSpec(memory_space=pl.ANY)] * 2,
        out_specs=pl.BlockSpec(memory_space=pl.ANY),
        scratch_shapes=[pltpu.VMEM((rows - large * count, wd.shape[1]), BF16), dma, dma((wd.shape[1] // COL,))],
        compiler_params=pltpu.CompilerParams(vmem_limit_bytes=8 * 2**20),
        name="lay_out",
    )(pltpu.with_memory_space_constraint(y, pltpu.HBM), pltpu.with_memory_space_constraint(v, pltpu.VMEM))


def solution(mesh):
    nt = mesh.shape["tp"]
    return jax.shard_map(
        functools.partial(block, nt, LARGE, COUNT),
        mesh=mesh,
        in_specs=(P("dp", None), P(None, "tp"), P(None, "tp"), P("tp", None)),
        out_specs=P("dp", None),
        check_vma=False,
    )
```

time: 1520 us -> 924 us (0.61)
  matrix products: 928 us -> 0 us
  Pallas kernels: 0 us -> 924 us
  waiting for transfers between devices: 560 us -> 0 us
  local copies, waits for them, and re-layouts: 23 us -> 0 us
    dot_general x3 -> x0, matrix products: 928 us -> none  [the longest x1 314 us: step(): up = jnp.dot(x, w_up, preferred_element_type=jnp.float32)]
    pallas_call x0 -> x2, Pallas kernels: none -> 924 us  [the longest x1 912 us: block(): pl.pallas_call(functools.partial(kernel, nt, large, count), out_shape=[ja...]
    psum x1 -> x0, waiting for transfers between devices: 560 us -> none  [step(): return lax.psum(term, 'tp')]
    unnamed x1 -> x0, local copies, waits for them, and re-layouts: 23 us -> none
  transfers between devices with their start and end apart: 1 -> 0, of which waited for: 1 -> 0; matrix products, arithmetic and copies ran while one was open for 0% -> 0% of each run, Pallas kernels for 0% -> 0%
where the time goes in v2:
time: 924 us
  Pallas kernels  924 us (100%)
    pallas_call x1, Pallas kernels, block(): pl.pallas_call(functools.partial(kernel, nt, large, count), out_shape=[ja...  912 us

profile of v2, /device:TPU:112, one launch (start us, length us, event | category | flops | bytes accessed | tf_op | source)
XLA Modules:
  0.0 923.9 jit_solution(8507394288585396184)
XLA Ops:
  0.0 911.7 %mlp_block.1 = (bf16[2048,8192]{1,0:T(8,128)(2,1)}, bf16[4,2,8192,256]{3,2,1,0:T(8,128)(2,1)S(1)}) custom-call(bf16[2048,8192]{1,0:T(8,128)(2,1)} %x.1, bf16[8192,8192]{1,0:T(8,128)(2,1)} %wg.1, bf16[8192,8192]{1,0:T(8,128)(2,1)} %wu.1, bf16[8192,8192]{1,0:T(8,128)(2,1)} %wd.1), custom_call_target="tpu_custom_call" | custom-call | tf_op jit(solution)/shard_map/mlp_block/pallas_call | solution.py:373
  911.7 12.1 %lay_out.1 = bf16[2048,8192]{1,0:T(8,128)(2,1)} custom-call(bf16[2048,8192]{1,0:T(8,128)(2,1)} %get-tuple-element.7.y, bf16[4,2,8192,256]{3,2,1,0:T(8,128)(2,1)S(1)} %get-tuple-element.8.v), custom_call_target="tpu_custom_call" | custom-call | tf_op jit(solution)/shard_map/lay_out/pallas_call | solution.py:390

commit v3 on v2

--- a/solution.py
+++ b/solution.py
@@ -131,9 +131,9 @@
         at = small_y(way, hop, b)
         return remote(way, at, at, sagsend.at[way, s], sagrecv.at[way, recv, b])
 
-    def products(lhs, t, beside):
+    def products(lhs, t, waits, beside):
         slot = lax.rem(t, SLOTS)
-        beside = [(K // COL // 4, lambda: w_start(t + 3)), (3 * (K // COL) // 4, lambda: w_wait(t + 1)), *beside]
+        beside = [(1, lambda: w_start(t + 3)), *((late, functools.partial(w_wait, t + 1 + n)) for n in range(waits)), *((late, act) for act in beside)]
         out = [None, None]
         for k in range(K // COL):
             at = pl.ds(k * COL, COL)
@@ -146,10 +146,10 @@
                     act()
         return out
 
-    mid = K // COL // 2
-
-    def gate_up(m, t, hs, j, *beside):
-        g, u = products(lambda at: xv[pl.ds(0, m), at], t, beside)
+    late = 3 * (K // COL) // 4
+
+    def gate_up(m, t, hs, j, waits, *beside):
+        g, u = products(lambda at: xv[pl.ds(0, m), at], t, waits, beside)
         hv[hs, pl.ds(0, m), pl.ds(pl.multiple_of(j * COL, COL), COL)] = (jax.nn.silu(g) * u).astype(BF16)
 
     def down_pair(t, hs, c, q, beside):
@@ -172,7 +172,7 @@
                     rs_copy(way, 0, came).wait_recv()
 
         for k in range(2):
-            both = products(lambda at: hv[hs, :, at], t + k, [(mid, ready)] if k == 0 else beside)
+            both = products(lambda at: hv[hs, :, at], t + k, 2 - 2 * k, [ready] if k == 0 else beside)
             at = pl.ds(k * COL, COL)
             for way in range(2):
                 v = both[way] + rsin[way, place, :, at].astype(F32)
@@ -223,18 +223,18 @@
             def x_wait():
                 pl.when(z == 0)(lambda: x_copy(0, large).wait())
 
-            down_pair(t, 1 - hs, i - 1, z, [(mid, x_wait)])
-            gate_up(large, t + 2, hs, 2 * z, (mid, lambda: send(i - 1, z)))
-            gate_up(large, t + 3, hs, 2 * z + 1)
+            down_pair(t, 1 - hs, i - 1, z, [x_wait])
+            gate_up(large, t + 2, hs, 2 * z, 2, lambda: send(i - 1, z))
+            gate_up(large, t + 3, hs, 2 * z + 1, 0)
 
         @pl.when(z >= drounds)
         def _():
             j = jnp.where(v < first, 4 * v, 4 * z - dn)
             ev = z - drounds
             on = (v >= first) & (ev < (nt - 2) * lag)
-            gate_up(large, t, hs, j, (mid, lambda: forward(i - 1, ev, on)))
+            gate_up(large, t, hs, j, 2, lambda: forward(i - 1, ev, on))
             for k in range(1, 4):
-                gate_up(large, t + k, hs, j + k)
+                gate_up(large, t + k, hs, j + k, 2 if k == 2 else 0)
 
         return 0
 
@@ -250,8 +250,8 @@
         def x_wait():
             pl.when(q == 0)(lambda: x_copy(0, small).wait())
 
-        down_pair(t, hs0, c0, q, [(mid, x_wait)])
-        gate_up(small, t + 2, hs1, q, (mid, lambda: send(c0, q)))
+        down_pair(t, hs0, c0, q, [x_wait])
+        gate_up(small, t + 2, hs1, q, 1, lambda: send(c0, q))
         return 0
 
     lax.fori_loop(0, drounds, mixed_steps, 0)
@@ -259,8 +259,8 @@
     def small_steps(n, _):
         j = drounds + 2 * n
         on = (lax.rem(n, 3) == 0) & (n // 3 < (nt - 2) * lag)
-        gate_up(small, t0 + dn + j, hs1, j, (mid, lambda: forward(c0, n // 3, on)))
-        gate_up(small, t0 + dn + j + 1, hs1, j + 1)
+        gate_up(small, t0 + dn + j, hs1, j, 1, lambda: forward(c0, n // 3, on))
+        gate_up(small, t0 + dn + j + 1, hs1, j + 1, 1)
         return 0
 
     lax.fori_loop(0, (gn - drounds) // 2, small_steps, 0)
@@ -288,7 +288,7 @@
                 def _():
                     small_rs(way, 0, h, came).wait_recv()
 
-        both = products(lambda at: hv[hs1, pl.ds(0, small), at], t0 + ds, [(3 * mid // 2, ready)])
+        both = products(lambda at: hv[hs1, pl.ds(0, small), at], t0 + ds, 1, [ready])
         for way in range(2):
             v = both[way] + rsin[way, place, pl.ds(0, small), half(h)].astype(F32)
             stg[way, s, pl.ds(0, small), half(h)] = v.astype(BF16)

time: 924 us -> 915 us (level)
  no operation moved by 1% of the time
where the time goes in v3:
time: 915 us
  Pallas kernels  915 us (100%)
    pallas_call x1, Pallas kernels, block(): pl.pallas_call(functools.partial(kernel, nt, large, count), out_shape=[ja...  903 us

profile of v3, /device:TPU:112, one launch (start us, length us, event | category | flops | bytes accessed | tf_op | source)
XLA Modules:
  0.0 914.8 jit_solution(7944237872759684616)
XLA Ops:
  0.0 902.5 %mlp_block.1 = (bf16[2048,8192]{1,0:T(8,128)(2,1)}, bf16[4,2,8192,256]{3,2,1,0:T(8,128)(2,1)S(1)}) custom-call(bf16[2048,8192]{1,0:T(8,128)(2,1)} %x.1, bf16[8192,8192]{1,0:T(8,128)(2,1)} %wg.1, bf16[8192,8192]{1,0:T(8,128)(2,1)} %wu.1, bf16[8192,8192]{1,0:T(8,128)(2,1)} %wd.1), custom_call_target="tpu_custom_call" | custom-call | tf_op jit(solution)/shard_map/mlp_block/pallas_call | solution.py:373
  902.5 12.1 %lay_out.1 = bf16[2048,8192]{1,0:T(8,128)(2,1)} custom-call(bf16[2048,8192]{1,0:T(8,128)(2,1)} %get-tuple-element.7.y, bf16[4,2,8192,256]{3,2,1,0:T(8,128)(2,1)S(1)} %get-tuple-element.8.v), custom_call_target="tpu_custom_call" | custom-call | tf_op jit(solution)/shard_map/lay_out/pallas_call | solution.py:390
